TPU v7x, 32 devices: a whole 2x2x4 slice. The times are simulated.
32 devices in a mesh: seq: 8 (over z, x), head: 4 (over y, core).
Axes of the slice: x: 2, y: 2, z: 4, core: 2. Of those that a mesh axis runs over, the one named last changes fastest.
Arguments:
- q_latent: bfloat16 [2048, 1536], P('seq', 'head'), may hold values from -6 to 6
- kv_latent: bfloat16 [2048, 512], P('seq', 'head'), may hold values from -6 to 6
- k_rope: bfloat16 [2048, 64], P('seq'), may hold values from -6 to 6
- segment_ids: int32 [2048], P('seq'), may hold values from 0 to 7, as said below
- w_q_nope: bfloat16 [1536, 16384], P('seq', 'head'), may hold values from -6 to 6
- w_q_rope: bfloat16 [1536, 8192], P('seq', 'head'), may hold values from -6 to 6
- w_kv_nope: bfloat16 [512, 16384], P('seq', 'head'), may hold values from -6 to 6
- threshold: float32 [1], replicated, may hold values from 3.5 to 5.5
Outputs:
- new_q_nope: bfloat16 [1536, 16384], P('seq', 'head')
- new_q_rope: bfloat16 [1536, 8192], P('seq', 'head')
- new_kv_nope: bfloat16 [512, 16384], P('seq', 'head')
- head_max: float32 [128], P('head')
- row_max: float32 [2048, 128], P('seq', 'head')
Inputs may be any that keep to these rules, and one draw needn't show every extreme that they name: segment_ids never fall along the tokens and each document has 1 to 768 tokens.
All inputs are finite; a program needn't handle non-finite values.
Results may differ from a plain program's by a relative error of at most 0.0034.
Values may be sent and summed in bfloat16 or wider, within the bound.
A program may use at most 128 MiB of HBM per device.

v0:
```python
import math
import jax
import jax.numpy as jnp
from jax import lax
from jax.sharding import PartitionSpec as P

D_NOPE = 128
D_ROPE = 64
QLORA = 1536
KVLORA = 512
REACH = 3


def as_sent(value):
    return jax.tree.map(lambda a: a.astype(jnp.bfloat16) if a.dtype == jnp.float32 else a, value)


def from_partner(value, axis, stride):
    mask = 2**stride
    pairs = [(source, source ^ mask) for source in range(lax.axis_size(axis))]
    return lax.ppermute(value, axis, pairs)


def shifted(block, axis, distance):
    devices = range(lax.axis_size(axis))
    route = [(i - distance, i) for i in devices if i - distance in devices]
    return lax.ppermute(block, axis, route)


def score_max(query_nope, query_rope, key_nope, key_rope, allowed):
    nope = jnp.einsum("qhd,khd->hqk", query_nope, key_nope, preferred_element_type=jnp.float32)
    rope = jnp.einsum("qhd,kd->hqk", query_rope, key_rope, preferred_element_type=jnp.float32)
    scores = (nope + rope) * (1.0 / math.sqrt(D_NOPE + D_ROPE))
    return jnp.max(jnp.where(allowed[None], scores, jnp.float32(-1e30)), axis=2)


def masked_max(compute, operands):
    return compute(*operands)


def spread_columns(weight, width, quarter, copies):
    pieces = weight.reshape(weight.shape[0], 4, quarter * width).transpose(1, 0, 2)
    return jnp.tile(pieces, (copies, 1, 1))


def body(q_latent, kv_latent, k_rope, segment_ids, w_q_nope, w_q_rope, w_kv_nope, threshold):
    q_whole, kv_whole = (
        lax.all_gather(q_latent, "head", axis=1, tiled=True),
        lax.all_gather(kv_latent, "head", axis=1, tiled=True),
    )
    rows = q_whole.shape[0]
    heads = w_q_nope.shape[1] // D_NOPE
    q_scale = 1.0 / math.sqrt(QLORA)
    k_scale = 1.0 / math.sqrt(KVLORA)
    place = lax.axis_index("seq")
    quarter = heads // 4
    copies = lax.axis_size("seq") // 4
    slot = place % 4
    sent = (
        spread_columns(w_q_nope, D_NOPE, quarter, copies),
        spread_columns(w_q_rope, D_ROPE, quarter, copies),
        spread_columns(w_kv_nope, D_NOPE, quarter, copies),
    )
    got_nope, got_rope, got_kv = (
        lax.all_to_all(sent[0], "seq", split_axis=0, concat_axis=1, tiled=True),
        lax.all_to_all(sent[1], "seq", split_axis=0, concat_axis=1, tiled=True),
        lax.all_to_all(sent[2], "seq", split_axis=0, concat_axis=1, tiled=True),
    )
    sub_nope = got_nope.reshape(QLORA, quarter * D_NOPE)
    sub_rope = got_rope.reshape(QLORA, quarter * D_ROPE)
    sub_kv = got_kv.reshape(KVLORA, quarter * D_NOPE)
    group = (q_whole, kv_whole, k_rope)
    for level in range(2):
        partner = jax.tree.map(
            lambda part, own: part.astype(own.dtype),
            from_partner(as_sent(group), "seq", level),
            group,
        )
        upper = place // (1 << level) % 2 == 1
        group = tuple(
            (
                jnp.where(
                    upper, jnp.concatenate([other, mine], 0), jnp.concatenate([mine, other], 0)
                )
                for mine, other in zip(group, partner)
            )
        )
    group_q, group_kv, group_rope = group
    early_kv, early_rope = shifted(
        (group_kv[(4 - REACH) * rows :], group_rope[(4 - REACH) * rows :]), "seq", 4
    )
    keys_kv = jnp.concatenate([early_kv, group_kv], 0)
    keys_rope = jnp.concatenate([early_rope, group_rope], 0)
    key_nope = (
        (jnp.dot(keys_kv, sub_kv, preferred_element_type=jnp.float32) * k_scale)
        .astype(jnp.bfloat16)
        .reshape(keys_kv.shape[0], quarter, D_NOPE)
    )
    query_nope = (
        (jnp.dot(group_q, sub_nope, preferred_element_type=jnp.float32) * q_scale)
        .astype(jnp.bfloat16)
        .reshape(4 * rows, quarter, D_NOPE)
    )
    query_rope = (
        (jnp.dot(group_q, sub_rope, preferred_element_type=jnp.float32) * q_scale)
        .astype(jnp.bfloat16)
        .reshape(4 * rows, quarter, D_ROPE)
    )
    all_segs = lax.all_gather(segment_ids, "seq", axis=0, tiled=True)
    padded_segs = jnp.concatenate([jnp.full((REACH * rows,), -1, jnp.int32), all_segs], 0)
    first = place // 4 * 4
    window = (REACH + 1) * rows
    block_rows = []
    for local in range(4):
        block = first + local
        query_seg = lax.dynamic_slice_in_dim(all_segs, block * rows, rows, 0)
        key_seg = lax.dynamic_slice_in_dim(padded_segs, block * rows, window, 0)
        query_pos = block * rows + jnp.arange(rows, dtype=jnp.int32)
        key_pos = (block - REACH) * rows + jnp.arange(window, dtype=jnp.int32)
        allowed = (
            (query_seg[:, None] == key_seg[None, :])
            & (key_pos[None, :] <= query_pos[:, None])
            & (key_pos[None, :] >= 0)
        )
        operands = (
            query_nope[local * rows : (local + 1) * rows],
            query_rope[local * rows : (local + 1) * rows],
            key_nope[local * rows : local * rows + window],
            keys_rope[local * rows : local * rows + window],
            allowed,
        )
        block_rows.append(masked_max(score_max, operands))
    stacked = jnp.stack(block_rows, 0)[None]
    for level in range(2):
        partner = from_partner(stacked, "seq", level)
        upper = place // (1 << level) % 2 == 1
        stacked = jnp.where(
            upper, jnp.concatenate([partner, stacked], 0), jnp.concatenate([stacked, partner], 0)
        )
    own = lax.dynamic_index_in_dim(stacked, slot, 1, False)
    row_max = own.reshape(heads, rows).T
    local_heads = jnp.max(row_max, axis=0)
    head_max = lax.pmax(local_heads, "seq")
    clip = threshold[0] / jnp.maximum(head_max, threshold[0])
    root = jnp.sqrt(clip)
    new_q_nope = (w_q_nope.astype(jnp.float32) * jnp.repeat(root, D_NOPE)[None, :]).astype(
        jnp.bfloat16
    )
    new_q_rope = (w_q_rope.astype(jnp.float32) * jnp.repeat(clip, D_ROPE)[None, :]).astype(
        jnp.bfloat16
    )
    new_kv_nope = (w_kv_nope.astype(jnp.float32) * jnp.repeat(root, D_NOPE)[None, :]).astype(
        jnp.bfloat16
    )
    return (new_q_nope, new_q_rope, new_kv_nope, head_max, row_max)


def solution(mesh):
    in_specs = (
        P("seq", "head"),
        P("seq", "head"),
        P("seq", None),
        P("seq"),
        P("seq", "head"),
        P("seq", "head"),
        P("seq", "head"),
        P(),
    )
    out_specs = (P("seq", "head"), P("seq", "head"), P("seq", "head"), P("head"), P("seq", "head"))
    return jax.shard_map(body, mesh=mesh, in_specs=in_specs, out_specs=out_specs, check_vma=False)
```

profile of v0, /device:TPU:0, one launch (start us, length us, event | category | flops | bytes accessed | tf_op | source)
XLA Modules:
  0.0 299.3 jit_solution(7385676597361516628)
XLA Ops:
  0.6 1.5 reshape.406
  2.2 0.2 copy.29
  2.3 1.1 tile.14
  3.4 7.3 %all-to-all-start.1 = ((bf16[8,64,1024]{2,1,0:T(8,128)(2,1)}), bf16[8,64,1024]{2,1,0:T(8,128)(2,1)S(1)}, u32[]{:S(2)}, u32[]{:S(2)}) async-start(bf16[8,64,1024]{2,1,0:T(8,128)(2,1)} %bitcast.8), calls=%async_computation.1 | async-start | bytes 2097152 | tf_op jit(solution)/shard_map/all_to_all | solution.py:67
  10.7 0.6 reshape.408
  11.3 0.1 copy.32
  11.4 25.0 %all-to-all-done.1 = bf16[8,64,1024]{2,1,0:T(8,128)(2,1)S(1)} async-done(((bf16[8,64,1024]{2,1,0:T(8,128)(2,1)}), bf16[8,64,1024]{2,1,0:T(8,128)(2,1)S(1)}, u32[]{:S(2)}, u32[]{:S(2)}) %all-to-all-start.1) | async-done | bytes 1048608 | tf_op jit(solution)/shard_map/all_to_all | solution.py:67
  36.5 1.4 tile.31
  37.9 4.3 %all-to-all-start.2 = ((bf16[8,192,512]{2,1,0:T(8,128)(2,1)}), bf16[8,192,512]{2,1,0:T(8,128)(2,1)}, u32[]{:S(2)}, u32[]{:S(2)}) async-start(bf16[8,192,512]{2,1,0:T(8,128)(2,1)} %bitcast.13), calls=%async_computation.2 | async-start | bytes 3145728 | tf_op jit(solution)/shard_map/all_to_all | solution.py:66
  42.3 1.2 reshape.404
  43.5 0.5 copy.28
  43.9 34.9 %all-to-all-done.2 = bf16[8,192,512]{2,1,0:T(8,128)(2,1)} async-done(((bf16[8,192,512]{2,1,0:T(8,128)(2,1)}), bf16[8,192,512]{2,1,0:T(8,128)(2,1)}, u32[]{:S(2)}, u32[]{:S(2)}) %all-to-all-start.2) | async-done | bytes 1572896 | tf_op jit(solution)/shard_map/all_to_all | solution.py:66
  78.8 2.1 tile.12
  81.0 4.6 %all-to-all-start = ((bf16[8,192,1024]{2,1,0:T(8,128)(2,1)}), bf16[8,192,1024]{2,1,0:T(8,128)(2,1)}, u32[]{:S(2)}, u32[]{:S(2)}) async-start(bf16[8,192,1024]{2,1,0:T(8,128)(2,1)} %bitcast.4), calls=%async_computation | async-start | bytes 6291456 | tf_op jit(solution)/shard_map/all_to_all | solution.py:65
  85.6 1.9 collective-permute-start.5
  87.5 5.8 %all_gather.11 = bf16[256,512]{1,0:T(8,128)(2,1)S(1)} all-gather(bf16[256,128]{1,0:T(8,128)(2,1)S(1)} %copy-done.15), channel_id=1, replica_groups=mesh['seq'=8,'head'=4] {'head'}, dimensions={1}, use_global_device_ids=true | all-gather | bytes 327680 | tf_op jit(solution)/shard_map/all_gather | solution.py:49
  93.3 0.2 collective-permute-start.2
  93.5 8.6 %all_gather.10 = bf16[256,1536]{1,0:T(8,128)(2,1)S(1)} all-gather(bf16[256,384]{1,0:T(8,128)(2,1)S(1)} %copy-done.14), channel_id=1, replica_groups=mesh['seq'=8,'head'=4] {'head'}, dimensions={1}, use_global_device_ids=true | all-gather | bytes 983040 | tf_op jit(solution)/shard_map/all_gather | solution.py:48
  102.1 1.8 collective-permute-start
  104.0 50.2 %all-gather = s32[8,1,256]{2,1,0:T(1,128)S(1)} all-gather(s32[1,1,256]{2,1,0:T(1,128)S(1)} %bitcast.118), channel_id=1, replica_groups=mesh['seq'=8,'head'=4] {'seq'}, dimensions={0}, use_global_device_ids=true | all-gather | bytes 9216 | tf_op jit(solution)/shard_map/all_gather | solution.py:109
  154.2 0.1 fusion.40
  154.3 0.1 pad_dynamic-slice_fusion.7
  154.4 0.2 maximum_select_fusion.5
  154.6 11.1 %collective-permute-start.3 = (bf16[512,512]{1,0:T(8,128)(2,1)S(1)}, bf16[512,512]{1,0:T(8,128)(2,1)S(1)}, u32[]{:S(2)}, u32[]{:S(2)}) collective-permute-start(bf16[512,512]{1,0:T(8,128)(2,1)S(1)} %maximum_select_fusion.5), channel_id=1, source_target_pairs={{0,8},{4,12},{8,0},{12,4},{16,24},{20,28},{24,16},{28,20},{1,9},{5... | collective-permute-start | bytes 1572872 | tf_op jit(solution)/shard_map/ppermute | solution.py:21
  165.7 0.3 and_and_fusion.3
  166.0 1.2 and_and_fusion.1
  167.3 6.2 %collective-permute-done.3 = bf16[512,512]{1,0:T(8,128)(2,1)S(1)} collective-permute-done((bf16[512,512]{1,0:T(8,128)(2,1)S(1)}, bf16[512,512]{1,0:T(8,128)(2,1)S(1)}, u32[]{:S(2)}, u32[]{:S(2)}) %collective-permute-start.3) | collective-permute-done | bytes 524320 | tf_op jit(solution)/shard_map/ppermute | solution.py:21
  173.5 0.5 maximum_select_fusion.2
  174.1 4.7 %collective-permute-start.4 = (bf16[768,512]{1,0:T(8,128)(2,1)S(1)}, bf16[768,512]{1,0:T(8,128)(2,1)S(1)}, u32[]{:S(2)}, u32[]{:S(2)}) collective-permute-start(bf16[768,512]{1,0:T(8,128)(2,1)S(1)} %slice.117), channel_id=1, source_target_pairs={{0,16},{4,20},{8,24},{12,28},{1,17},{5,21},{9,25},{13,29},{2,18},{... | collective-permute-start | bytes 2359304 | tf_op jit(solution)/shard_map/ppermute | solution.py:27
  178.8 0.6 maximum_select_fusion.1
  179.4 0.6 collective-permute-start.1
  180.1 1.5 collective-permute-start.6
  181.6 0.3 and_and_fusion
  182.0 44.8 %collective-permute-done.6 = bf16[512,64]{0,1:T(8,128)(2,1)S(1)} collective-permute-done((bf16[512,64]{0,1:T(8,128)(2,1)S(1)}, bf16[512,64]{0,1:T(8,128)(2,1)S(1)}, u32[]{:S(2)}, u32[]{:S(2)}) %collective-permute-start.6) | collective-permute-done | bytes 65568 | tf_op jit(solution)/shard_map/ppermute | solution.py:21
  226.8 0.6 slice.119
  227.4 2.1 collective-permute-start.7
  229.6 2.2 multiply_convert_fusion
  231.8 3.0 fusion.37
  234.7 3.9 %multiply_convert_fusion.3 = bf16[1024,512]{0,1:T(8,128)(2,1)S(1)} fusion(bf16[1536,512]{1,0:T(8,128)(2,1)} %bitcast.14, bf16[512,1536]{1,0:T(8,128)(2,1)S(1)} %maximum_select_fusion.1, bf16[512,1536]{1,0:T(8,128)(2,1)S(1)} %collective-permute-done.1, pred[]{:T(512)S(6)} %eq.82), kind=kOutput, calls=%fused_computation.20 | convolution fusion | flops 1625817088 | bytes 5767169 | tf_op jit(solution)/shard_map/dot_general | solution.py:105
  238.6 0.9 fusion.39
  239.5 7.3 %multiply_convert_fusion.1 = bf16[1024,1024]{0,1:T(8,128)(2,1)S(1)} fusion(bf16[1536,1024]{1,0:T(8,128)(2,1)} %bitcast.5, bf16[512,1536]{1,0:T(8,128)(2,1)} %copy-done.8, bf16[512,1536]{1,0:T(8,128)(2,1)} %copy-done.19, pred[]{:T(512)S(6)} %eq.82), kind=kOutput, calls=%fused_computation.17 | convolution fusion | flops 3237478400 | bytes 8388609 | tf_op jit(solution)/shard_map/dot_general | solution.py:100
  246.8 0.1 fusion.38
  246.9 1.4 copy-done.2
  248.4 1.3 fusion.44
  249.7 0.3 copy-done.1
  250.0 1.3 fusion.41
  251.2 0.3 copy-done
  251.5 1.3 fusion.43
  252.9 2.1 fusion.2
  255.0 1.5 fusion.42
  256.5 3.0 %fusion.11 = f32[8,256]{1,0:T(8,128)S(1)} fusion(f32[8,256,1024]{2,1,0:T(8,128)S(1)} %fusion.41, pred[256,1024]{1,0:T(8,128)(4,1)S(1)} %and_and_fusion.3, bf16[256,8,64]{0,2,1:T(8,128)(2,1)S(1)} %bitcast.109, bf16[1024,64]{0,1:T(8,128)(2,1)S(1)} %maximum_select_fusion.6, bf16[768,64]{0,1:T(8,128)(2,1)} %collective-permute-done.7), kind=kOutput, calls=%fused_computation.15 | convolution fusion | flops 277084160 | bytes 9150464 | tf_op jit(solution)/shard_map/qhd,kd->hqk/dot_general | solution.py:32
  259.6 2.9 fusion.5
  262.5 3.1 %fusion.8 = f32[8,256]{1,0:T(8,128)S(1)} fusion(f32[8,256,1024]{2,1,0:T(8,128)S(1)} %fusion.42, pred[256,1024]{1,0:T(8,128)(4,1)S(1)} %get-tuple-element.30, bf16[256,8,64]{0,2,1:T(8,128)(2,1)S(1)} %bitcast.107, bf16[1024,64]{0,1:T(8,128)(2,1)S(1)} %maximum_select_fusion.6, bf16[768,64]{0,1:T(8,128)(2,1)} %collective-permute-done.7), kind=kOutput, calls=%fused_computation.11 | convolution fusion | flops 277084160 | bytes 9150464 | tf_op jit(solution)/shard_map/qhd,kd->hqk/dot_general | solution.py:32
  265.7 3.4 %collective-permute-start.8 = (f32[1,4,8,256]{3,2,0,1:T(8,128)S(1)}, f32[1,4,8,256]{3,2,0,1:T(8,128)S(1)}, u32[]{:S(2)}, u32[]{:S(2)}) collective-permute-start(f32[1,4,8,256]{3,2,0,1:T(8,128)S(1)} %maximum_bitcast_fusion), channel_id=1, source_target_pairs={{0,4},{4,0},{8,12},{12,8},{16,20},{20,16},{24,28},{28,24},{1,5},{5... | collective-permute-start | bytes 98312 | tf_op jit(solution)/shard_map/ppermute | solution.py:21
  269.1 1.9 collective-permute-done.8
  271.0 2.5 collective-permute-start.9
  274.2 1.6 collective-permute-done.9
  275.8 0.6 fusion.35
  276.4 0.1 reduce_max.52
  276.5 19.1 %pmax.7 = f32[32]{0:T(128)S(1)} all-reduce(f32[32]{0:T(128)S(1)} %reduce_max.52), channel_id=1, replica_groups=mesh['seq'=8,'head'=4] {'seq'}, use_global_device_ids=true, to_apply=%region_5.6 | all-reduce | flops 32 | bytes 256 | tf_op jit(solution)/shard_map/pmax | solution.py:143
  295.7 0.1 broadcast_bitcast_fusion
  295.7 0.9 multiply_convert_fusion.5
  296.6 1.5 multiply_convert_fusion.2
  298.2 1.0 multiply_convert_fusion.4
  (64 shorter events, 0.5 us)
Async XLA Ops:
  0.6 10.1 %copy-start.5 = (bf16[192,2048]{1,0:T(8,128)(2,1)S(1)}, bf16[192,2048]{1,0:T(8,128)(2,1)}, u32[]{:S(2)}) copy-start(bf16[192,2048]{1,0:T(8,128)(2,1)} %param.13) | copy-start | bytes 2359300
  3.4 33.0 %all-to-all-start.1 = ((bf16[8,64,1024]{2,1,0:T(8,128)(2,1)}), bf16[8,64,1024]{2,1,0:T(8,128)(2,1)S(1)}, u32[]{:S(2)}, u32[]{:S(2)}) async-start(bf16[8,64,1024]{2,1,0:T(8,128)(2,1)} %bitcast.8), calls=%async_computation.1 | async-start | bytes 2097152 | tf_op jit(solution)/shard_map/all_to_all | solution.py:67
  11.4 30.8 %copy-start.3 = (bf16[192,4096]{1,0:T(8,128)(2,1)S(1)}, bf16[192,4096]{1,0:T(8,128)(2,1)}, u32[]{:S(2)}) copy-start(bf16[192,4096]{1,0:T(8,128)(2,1)} %param.12) | copy-start | bytes 4718596
  36.5 1.5 copy-start.9
  37.9 40.9 %all-to-all-start.2 = ((bf16[8,192,512]{2,1,0:T(8,128)(2,1)}), bf16[8,192,512]{2,1,0:T(8,128)(2,1)}, u32[]{:S(2)}, u32[]{:S(2)}) async-start(bf16[8,192,512]{2,1,0:T(8,128)(2,1)} %bitcast.13), calls=%async_computation.2 | async-start | bytes 3145728 | tf_op jit(solution)/shard_map/all_to_all | solution.py:66
  80.9 4.6 %copy-start.16 = (bf16[256,64]{0,1:T(8,128)(2,1)S(1)}, bf16[256,64]{0,1:T(8,128)(2,1)}, u32[]{:S(2)}) copy-start(bf16[256,64]{0,1:T(8,128)(2,1)} %param.10) | copy-start | bytes 98308
  80.9 6.5 %copy-start.15 = (bf16[256,128]{1,0:T(8,128)(2,1)S(1)}, bf16[256,128]{1,0:T(8,128)(2,1)}, u32[]{:S(2)}) copy-start(bf16[256,128]{1,0:T(8,128)(2,1)} %param.9) | copy-start | bytes 196612
  80.9 12.5 %copy-start.14 = (bf16[256,384]{1,0:T(8,128)(2,1)S(1)}, bf16[256,384]{1,0:T(8,128)(2,1)}, u32[]{:S(2)}) copy-start(bf16[256,384]{1,0:T(8,128)(2,1)} %param.8) | copy-start | bytes 589828
  81.0 23.1 %copy-start.17 = (s32[256]{0:T(256)S(1)}, s32[256]{0:T(256)}, u32[]{:S(2)}) copy-start(s32[256]{0:T(256)} %param.11) | copy-start | bytes 3076
  81.0 158.5 %all-to-all-start = ((bf16[8,192,1024]{2,1,0:T(8,128)(2,1)}), bf16[8,192,1024]{2,1,0:T(8,128)(2,1)}, u32[]{:S(2)}, u32[]{:S(2)}) async-start(bf16[8,192,1024]{2,1,0:T(8,128)(2,1)} %bitcast.4), calls=%async_computation | async-start | bytes 6291456 | tf_op jit(solution)/shard_map/all_to_all | solution.py:65
  85.6 94.5 %collective-permute-start.5 = (bf16[256,64]{0,1:T(8,128)(2,1)S(1)}, bf16[256,64]{0,1:T(8,128)(2,1)S(1)}, u32[]{:S(2)}, u32[]{:S(2)}) collective-permute-start(bf16[256,64]{0,1:T(8,128)(2,1)S(1)} %copy-done.16), channel_id=1, source_target_pairs={{0,4},{4,0},{8,12},{12,8},{16,20},{20,16},{24,28},{28,24},{1,5},{5... | collective-permute-start | bytes 98312 | tf_op jit(solution)/shard_map/ppermute | solution.py:21
  93.3 61.1 %collective-permute-start.2 = (bf16[256,512]{1,0:T(8,128)(2,1)S(1)}, bf16[256,512]{1,0:T(8,128)(2,1)S(1)}, u32[]{:S(2)}, u32[]{:S(2)}) collective-permute-start(bf16[256,512]{1,0:T(8,128)(2,1)S(1)} %all_gather.11), channel_id=1, source_target_pairs={{0,4},{4,0},{8,12},{12,8},{16,20},{20,16},{24,28},{28,24},{1,5},{5... | collective-permute-start | bytes 786440 | tf_op jit(solution)/shard_map/ppermute | solution.py:21
  102.1 76.7 %collective-permute-start = (bf16[256,1536]{1,0:T(8,128)(2,1)S(1)}, bf16[256,1536]{1,0:T(8,128)(2,1)S(1)}, u32[]{:S(2)}, u32[]{:S(2)}) collective-permute-start(bf16[256,1536]{1,0:T(8,128)(2,1)S(1)} %all_gather.10), channel_id=1, source_target_pairs={{0,4},{4,0},{8,12},{12,8},{16,20},{20,16},{24,28},{28,24},{1,5},{5... | collective-permute-start | bytes 2359304 | tf_op jit(solution)/shard_map/ppermute | solution.py:21
  154.6 18.9 %collective-permute-start.3 = (bf16[512,512]{1,0:T(8,128)(2,1)S(1)}, bf16[512,512]{1,0:T(8,128)(2,1)S(1)}, u32[]{:S(2)}, u32[]{:S(2)}) collective-permute-start(bf16[512,512]{1,0:T(8,128)(2,1)S(1)} %maximum_select_fusion.5), channel_id=1, source_target_pairs={{0,8},{4,12},{8,0},{12,4},{16,24},{20,28},{24,16},{28,20},{1,9},{5... | collective-permute-start | bytes 1572872 | tf_op jit(solution)/shard_map/ppermute | solution.py:21
  174.0 55.6 %copy-start.10 = (bf16[8,64,1024]{2,1,0:T(8,128)(2,1)S(1)}, bf16[8,64,1024]{2,1,0:T(8,128)(2,1)}, u32[]{:S(2)}) copy-start(bf16[8,64,1024]{2,1,0:T(8,128)(2,1)} %copy-done.9) | copy-start | bytes 3145732
  174.1 55.5 %collective-permute-start.4 = (bf16[768,512]{1,0:T(8,128)(2,1)S(1)}, bf16[768,512]{1,0:T(8,128)(2,1)S(1)}, u32[]{:S(2)}, u32[]{:S(2)}) collective-permute-start(bf16[768,512]{1,0:T(8,128)(2,1)S(1)} %slice.117), channel_id=1, source_target_pairs={{0,16},{4,20},{8,24},{12,28},{1,17},{5,21},{9,25},{13,29},{2,18},{... | collective-permute-start | bytes 2359304 | tf_op jit(solution)/shard_map/ppermute | solution.py:27
  179.4 55.3 %copy-start.8 = (bf16[512,1536]{1,0:T(8,128)(2,1)}, bf16[512,1536]{1,0:T(8,128)(2,1)S(1)}, u32[]{:S(2)}) copy-start(bf16[512,1536]{1,0:T(8,128)(2,1)S(1)} %maximum_select_fusion.1) | copy-start | bytes 4718596
  179.4 55.3 %collective-permute-start.1 = (bf16[512,1536]{1,0:T(8,128)(2,1)S(1)}, bf16[512,1536]{1,0:T(8,128)(2,1)S(1)}, u32[]{:S(2)}, u32[]{:S(2)}) collective-permute-start(bf16[512,1536]{1,0:T(8,128)(2,1)S(1)} %maximum_select_fusion.1), channel_id=1, source_target_pairs={{0,8},{4,12},{8,0},{12,4},{16,24},{20,28},{24,16},{28,20},{1,9},{5... | collective-permute-start | bytes 4718600 | tf_op jit(solution)/shard_map/ppermute | solution.py:21
  180.1 46.6 %collective-permute-start.6 = (bf16[512,64]{0,1:T(8,128)(2,1)S(1)}, bf16[512,64]{0,1:T(8,128)(2,1)S(1)}, u32[]{:S(2)}, u32[]{:S(2)}) collective-permute-start(bf16[512,64]{0,1:T(8,128)(2,1)S(1)} %maximum_select_fusion.7), channel_id=1, source_target_pairs={{0,8},{4,12},{8,0},{12,4},{16,24},{20,28},{24,16},{28,20},{1,9},{5... | collective-permute-start | bytes 196616 | tf_op jit(solution)/shard_map/ppermute | solution.py:21
  227.4 29.1 %collective-permute-start.7 = (bf16[768,64]{0,1:T(8,128)(2,1)}, bf16[768,64]{0,1:T(8,128)(2,1)}, u32[]{:S(2)}, u32[]{:S(2)}) collective-permute-start(bf16[768,64]{0,1:T(8,128)(2,1)} %slice.119), channel_id=1, source_target_pairs={{0,16},{4,20},{8,24},{12,28},{1,17},{5,21},{9,25},{13,29},{2,18},{... | collective-permute-start | bytes 294920 | tf_op jit(solution)/shard_map/ppermute | solution.py:27
  234.7 3.9 %copy-start.19 = (bf16[512,1536]{1,0:T(8,128)(2,1)}, bf16[512,1536]{1,0:T(8,128)(2,1)S(1)}, u32[]{:S(2)}) copy-start(bf16[512,1536]{1,0:T(8,128)(2,1)S(1)} %collective-permute-done.1) | copy-start | bytes 4718596
  246.8 1.6 copy-start.2
  248.4 1.6 copy-start.1
  250.0 1.6 copy-start
  251.5 1.3 copy-start.13
  256.5 3.1 %copy-start.11 = (pred[256,1024]{1,0:T(8,128)(4,1)S(1)}, pred[256,1024]{1,0:T(8,128)(4,1)}, u32[]{:S(2)}) copy-start(pred[256,1024]{1,0:T(8,128)(4,1)} %get-tuple-element.29) | copy-start | bytes 786436
  259.6 2.9 copy-start.12
  262.5 33.2 %copy-start.7 = (bf16[64,4096]{1,0:T(8,128)(2,1)S(1)}, bf16[64,4096]{1,0:T(8,128)(2,1)}, u32[]{:S(2)}) copy-start(bf16[64,4096]{1,0:T(8,128)(2,1)} %param.14) | copy-start | bytes 1572868
  262.5 34.1 %copy-start.4 = (bf16[192,4096]{1,0:T(8,128)(2,1)S(1)}, bf16[192,4096]{1,0:T(8,128)(2,1)}, u32[]{:S(2)}) copy-start(bf16[192,4096]{1,0:T(8,128)(2,1)} %param.12) | copy-start | bytes 4718596
  265.7 32.6 %copy-start.6 = (bf16[192,2048]{1,0:T(8,128)(2,1)S(1)}, bf16[192,2048]{1,0:T(8,128)(2,1)}, u32[]{:S(2)}) copy-start(bf16[192,2048]{1,0:T(8,128)(2,1)} %param.13) | copy-start | bytes 2359300
  265.7 5.3 %collective-permute-start.8 = (f32[1,4,8,256]{3,2,0,1:T(8,128)S(1)}, f32[1,4,8,256]{3,2,0,1:T(8,128)S(1)}, u32[]{:S(2)}, u32[]{:S(2)}) collective-permute-start(f32[1,4,8,256]{3,2,0,1:T(8,128)S(1)} %maximum_bitcast_fusion), channel_id=1, source_target_pairs={{0,4},{4,0},{8,12},{12,8},{16,20},{20,16},{24,28},{28,24},{1,5},{5... | collective-permute-start | bytes 98312 | tf_op jit(solution)/shard_map/ppermute | solution.py:21
  271.0 4.8 %collective-permute-start.9 = (f32[2,4,8,256]{3,2,0,1:T(8,128)S(1)}, f32[2,4,8,256]{3,2,0,1:T(8,128)S(1)}, u32[]{:S(2)}, u32[]{:S(2)}) collective-permute-start(f32[2,4,8,256]{3,2,0,1:T(8,128)S(1)} %maximum_select_fusion.8), channel_id=1, source_target_pairs={{0,8},{4,12},{8,0},{12,4},{16,24},{20,28},{24,16},{28,20},{1,9},{5... | collective-permute-start | bytes 196616 | tf_op jit(solution)/shard_map/ppermute | solution.py:21
  295.6 3.6 %copy-start.18 = (f32[32]{0:T(128)}, f32[32]{0:T(128)S(1)}, u32[]{:S(2)}) copy-start(f32[32]{0:T(128)S(1)} %pmax.7) | copy-start | bytes 388
where the time goes:
time: 300 us; the launch traced here: 299 us
  waiting for transfers between devices  114 us (38%)
  blocking collectives  83.7 us (28%)
  starting transfers between devices  46.2 us (15%)
  matrix products  29.9 us (10%)
  local copies, waits for them, and re-layouts  16 us (5%)
  other arithmetic  7.27 us (2%)
    ppermute x8, waiting for transfers between devices, from_partner(): return lax.ppermute(value, axis, pairs)  54.5 us
    all_gather x1, blocking collectives, body(): all_segs = lax.all_gather(segment_ids, 'seq', axis=0, tiled=True)  50.2 us
    all_to_all x1, waiting for transfers between devices, body(): lax.all_to_all(sent[1], 'seq', split_axis=0, concat_axis=1, tiled=True)  34.9 us
    all_to_all x1, waiting for transfers between devices, body(): lax.all_to_all(sent[2], 'seq', split_axis=0, concat_axis=1, tiled=True)  25 us
    ppermute x8, starting transfers between devices, from_partner(): return lax.ppermute(value, axis, pairs)  23.1 us
    pmax x1, blocking collectives, body(): head_max = lax.pmax(local_heads, 'seq')  19.1 us
    dot_general x4, matrix products, score_max(): jnp.einsum('qhd,kd->hqk', query_rope, key_rope, preferred_element_type=jn...  11.2 us
    all_gather x1, blocking collectives, body(): lax.all_gather(q_latent, 'head', axis=1, tiled=True)  8.59 us
  transfers between devices with their start and end apart: 13, of which 6 were waited for; matrix products, arithmetic and copies ran while one was open for 10% of the time, Pallas kernels for 0%

commit v1 on v0

--- a/solution.py
+++ b/solution.py
@@ -106,7 +106,9 @@
         .astype(jnp.bfloat16)
         .reshape(4 * rows, quarter, D_ROPE)
     )
-    all_segs = lax.all_gather(segment_ids, "seq", axis=0, tiled=True)
+    all_segs = jnp.concatenate(
+        lax.all_to_all(jnp.stack([segment_ids] * lax.axis_size("seq")), "seq", 0, 0), axis=0
+    )
     padded_segs = jnp.concatenate([jnp.full((REACH * rows,), -1, jnp.int32), all_segs], 0)
     first = place // 4 * 4
     window = (REACH + 1) * rows

time: 300 us -> 287 us (0.957)
  blocking collectives: 83.7 us -> 32.2 us
  waiting for transfers between devices: 114 us -> 158 us
  starting transfers between devices: 46.2 us -> 41.1 us
    all_gather x1 -> x0, blocking collectives: 50.2 us -> none  [body(): all_segs = lax.all_gather(segment_ids, 'seq', axis=0, tiled=True)]
    ppermute x8, waiting for transfers between devices: 54.5 us -> 94.2 us  [from_partner(): return lax.ppermute(value, axis, pairs)]
    ppermute x8, starting transfers between devices: 23.1 us -> 9.44 us  [from_partner(): return lax.ppermute(value, axis, pairs)]
    all_to_all x0 -> x1, starting transfers between devices: none -> 7.28 us  [body(): lax.all_to_all(jnp.stack([segment_ids] * lax.axis_size('seq')), 'seq', 0, 0)]
    ppermute x2, starting transfers between devices: 6.85 us -> 11.9 us  [shifted(): return lax.ppermute(block, axis, route)]
    all_to_all x0 -> x1, waiting for transfers between devices: none -> 4.92 us  [body(): lax.all_to_all(jnp.stack([segment_ids] * lax.axis_size('seq')), 'seq', 0, 0)]
    all_to_all x1, starting transfers between devices: 7.28 us -> 3.56 us  [body(): lax.all_to_all(sent[2], 'seq', split_axis=0, concat_axis=1, tiled=True)]
  transfers between devices with their start and end apart: 13 -> 14, of which waited for: 6 -> 8; matrix products, arithmetic and copies ran while one was open for 10% -> 11% of each run, Pallas kernels for 0% -> 0%
where the time goes in v1:
time: 287 us
  waiting for transfers between devices  158 us (55%)
  starting transfers between devices  41.1 us (14%)
  blocking collectives  32.2 us (11%)
  matrix products  29.9 us (10%)
  local copies, waits for them, and re-layouts  17.3 us (6%)
  other arithmetic  6.63 us (2%)
    ppermute x8, waiting for transfers between devices, from_partner(): return lax.ppermute(value, axis, pairs)  94.2 us
    all_to_all x1, waiting for transfers between devices, body(): lax.all_to_all(sent[1], 'seq', split_axis=0, concat_axis=1, tiled=True)  34.7 us
    all_to_all x1, waiting for transfers between devices, body(): lax.all_to_all(sent[2], 'seq', split_axis=0, concat_axis=1, tiled=True)  24 us
    pmax x1, blocking collectives, body(): head_max = lax.pmax(local_heads, 'seq')  17.8 us
    ppermute x2, starting transfers between devices, shifted(): return lax.ppermute(block, axis, route)  11.9 us
    dot_general x4, matrix products, score_max(): jnp.einsum('qhd,kd->hqk', query_rope, key_rope, preferred_element_type=jn...  11.2 us
    ppermute x8, starting transfers between devices, from_partner(): return lax.ppermute(value, axis, pairs)  9.44 us
    all_gather x1, blocking collectives, body(): lax.all_gather(q_latent, 'head', axis=1, tiled=True)  8.59 us
  transfers between devices with their start and end apart: 14, of which 8 were waited for; matrix products, arithmetic and copies ran while one was open for 11% of the time, Pallas kernels for 0%

profile of v1, /device:TPU:0, one launch (start us, length us, event | category | flops | bytes accessed | tf_op | source)
XLA Modules:
  0.0 286.7 jit_solution(16926881100023622073)
XLA Ops:
  0.6 1.4 stack.12
  2.0 7.3 %all-to-all-start = ((s32[8,1,256]{2,1,0:T(1,128)}), s32[8,1,256]{2,1,0:T(1,128)S(1)}, u32[]{:S(2)}, u32[]{:S(2)}) async-start(s32[8,1,256]{2,1,0:T(1,128)} %stack.12), calls=%async_computation | async-start | bytes 16384 | tf_op jit(solution)/shard_map/all_to_all | solution.py:110
  9.3 1.4 reshape.418
  10.7 0.2 copy.14
  10.9 4.9 %all-to-all-done = s32[8,1,256]{2,1,0:T(1,128)S(1)} async-done(((s32[8,1,256]{2,1,0:T(1,128)}), s32[8,1,256]{2,1,0:T(1,128)S(1)}, u32[]{:S(2)}, u32[]{:S(2)}) %all-to-all-start) | async-done | bytes 8224 | tf_op jit(solution)/shard_map/all_to_all | solution.py:110
  15.8 1.1 tile.14
  16.9 3.6 %all-to-all-start.2 = ((bf16[8,64,1024]{2,1,0:T(8,128)(2,1)}), bf16[8,64,1024]{2,1,0:T(8,128)(2,1)S(1)}, u32[]{:S(2)}, u32[]{:S(2)}) async-start(bf16[8,64,1024]{2,1,0:T(8,128)(2,1)} %bitcast.7), calls=%async_computation.2 | async-start | bytes 2097152 | tf_op jit(solution)/shard_map/all_to_all | solution.py:67
  20.5 0.6 reshape.420
  21.1 0.1 copy.17
  21.2 24.0 %all-to-all-done.2 = bf16[8,64,1024]{2,1,0:T(8,128)(2,1)S(1)} async-done(((bf16[8,64,1024]{2,1,0:T(8,128)(2,1)}), bf16[8,64,1024]{2,1,0:T(8,128)(2,1)S(1)}, u32[]{:S(2)}, u32[]{:S(2)}) %all-to-all-start.2) | async-done | bytes 1048608 | tf_op jit(solution)/shard_map/all_to_all | solution.py:67
  45.2 1.4 tile.31
  46.7 4.3 %all-to-all-start.3 = ((bf16[8,192,512]{2,1,0:T(8,128)(2,1)}), bf16[8,192,512]{2,1,0:T(8,128)(2,1)}, u32[]{:S(2)}, u32[]{:S(2)}) async-start(bf16[8,192,512]{2,1,0:T(8,128)(2,1)} %bitcast.12), calls=%async_computation.3 | async-start | bytes 3145728 | tf_op jit(solution)/shard_map/all_to_all | solution.py:66
  51.0 1.2 reshape.416
  52.2 0.5 copy.13
  52.7 34.7 %all-to-all-done.3 = bf16[8,192,512]{2,1,0:T(8,128)(2,1)} async-done(((bf16[8,192,512]{2,1,0:T(8,128)(2,1)}), bf16[8,192,512]{2,1,0:T(8,128)(2,1)}, u32[]{:S(2)}, u32[]{:S(2)}) %all-to-all-start.3) | async-done | bytes 1572896 | tf_op jit(solution)/shard_map/all_to_all | solution.py:66
  87.4 2.1 tile.12
  89.5 4.6 %all-to-all-start.1 = ((bf16[8,192,1024]{2,1,0:T(8,128)(2,1)}), bf16[8,192,1024]{2,1,0:T(8,128)(2,1)}, u32[]{:S(2)}, u32[]{:S(2)}) async-start(bf16[8,192,1024]{2,1,0:T(8,128)(2,1)} %bitcast.3), calls=%async_computation.1 | async-start | bytes 6291456 | tf_op jit(solution)/shard_map/all_to_all | solution.py:65
  94.1 1.9 collective-permute-start.5
  96.0 5.8 %all_gather.7 = bf16[256,512]{1,0:T(8,128)(2,1)S(1)} all-gather(bf16[256,128]{1,0:T(8,128)(2,1)S(1)} %copy-done.15), channel_id=1, replica_groups=mesh['seq'=8,'head'=4] {'head'}, dimensions={1}, use_global_device_ids=true | all-gather | bytes 327680 | tf_op jit(solution)/shard_map/all_gather | solution.py:49
  101.8 0.2 collective-permute-start.2
  102.0 8.6 %all_gather.6 = bf16[256,1536]{1,0:T(8,128)(2,1)S(1)} all-gather(bf16[256,384]{1,0:T(8,128)(2,1)S(1)} %copy-done.14), channel_id=1, replica_groups=mesh['seq'=8,'head'=4] {'head'}, dimensions={1}, use_global_device_ids=true | all-gather | bytes 983040 | tf_op jit(solution)/shard_map/all_gather | solution.py:48
  110.6 1.8 collective-permute-start
  112.6 15.3 %collective-permute-done.2 = bf16[256,512]{1,0:T(8,128)(2,1)S(1)} collective-permute-done((bf16[256,512]{1,0:T(8,128)(2,1)S(1)}, bf16[256,512]{1,0:T(8,128)(2,1)S(1)}, u32[]{:S(2)}, u32[]{:S(2)}) %collective-permute-start.2) | collective-permute-done | bytes 262176 | tf_op jit(solution)/shard_map/ppermute | solution.py:21
  128.0 0.2 maximum_select_fusion.5
  128.3 0.1 fusion.40
  128.4 0.1 pad_dynamic-slice_fusion.7
  128.5 0.6 and_and_fusion.1
  129.1 27.2 %collective-permute-done.3 = bf16[512,512]{1,0:T(8,128)(2,1)S(1)} collective-permute-done((bf16[512,512]{1,0:T(8,128)(2,1)S(1)}, bf16[512,512]{1,0:T(8,128)(2,1)S(1)}, u32[]{:S(2)}, u32[]{:S(2)}) %collective-permute-start.3) | collective-permute-done | bytes 524320 | tf_op jit(solution)/shard_map/ppermute | solution.py:21
  156.3 0.5 maximum_select_fusion.2
  156.8 6.0 %collective-permute-start.4 = (bf16[768,512]{1,0:T(8,128)(2,1)S(1)}, bf16[768,512]{1,0:T(8,128)(2,1)S(1)}, u32[]{:S(2)}, u32[]{:S(2)}) collective-permute-start(bf16[768,512]{1,0:T(8,128)(2,1)S(1)} %slice.117), channel_id=1, source_target_pairs={{0,16},{4,20},{8,24},{12,28},{1,17},{5,21},{9,25},{13,29},{2,18},{... | collective-permute-start | bytes 2359304 | tf_op jit(solution)/shard_map/ppermute | solution.py:27
  162.8 0.6 maximum_select_fusion.1
  163.5 0.3 and_and_fusion.3
  163.9 2.1 collective-permute-start.6
  165.9 0.3 and_and_fusion
  166.3 46.8 %collective-permute-done.6 = bf16[512,64]{0,1:T(8,128)(2,1)S(1)} collective-permute-done((bf16[512,64]{0,1:T(8,128)(2,1)S(1)}, bf16[512,64]{0,1:T(8,128)(2,1)S(1)}, u32[]{:S(2)}, u32[]{:S(2)}) %collective-permute-start.6) | collective-permute-done | bytes 65568 | tf_op jit(solution)/shard_map/ppermute | solution.py:21
  213.1 0.6 slice.119
  213.7 6.0 %collective-permute-start.7 = (bf16[768,64]{0,1:T(8,128)(2,1)}, bf16[768,64]{0,1:T(8,128)(2,1)}, u32[]{:S(2)}, u32[]{:S(2)}) collective-permute-start(bf16[768,64]{0,1:T(8,128)(2,1)} %slice.119), channel_id=1, source_target_pairs={{0,16},{4,20},{8,24},{12,28},{1,17},{5,21},{9,25},{13,29},{2,18},{... | collective-permute-start | bytes 294920 | tf_op jit(solution)/shard_map/ppermute | solution.py:27
  219.7 2.2 multiply_convert_fusion
  221.9 2.9 %fusion.37 = (bf16[1024,1024]{0,1:T(8,128)(2,1)}, bf16[1024,1024]{0,1:T(8,128)(2,1)}, bf16[1024,1024]{0,1:T(8,128)(2,1)}, bf16[1024,1024]{0,1:T(8,128)(2,1)S(1)}) fusion(bf16[1792,1024]{0,1:T(8,128)(2,1)S(1)} %multiply_convert_fusion), kind=kLoop, calls=%fused_computation.82 | loop fusion | bytes 16777216 | tf_op jit(solution)/shard_map/slice | solution.py:130
  224.8 3.9 %multiply_convert_fusion.3 = bf16[1024,512]{0,1:T(8,128)(2,1)S(1)} fusion(bf16[1536,512]{1,0:T(8,128)(2,1)} %bitcast.13, bf16[512,1536]{1,0:T(8,128)(2,1)S(1)} %maximum_select_fusion.1, bf16[512,1536]{1,0:T(8,128)(2,1)S(1)} %collective-permute-done.1, pred[]{:T(512)S(6)} %eq.82), kind=kOutput, calls=%fused_computation.20 | convolution fusion | flops 1625817088 | bytes 5767169 | tf_op jit(solution)/shard_map/dot_general | solution.py:105
  228.7 0.9 fusion.39
  229.7 7.2 %multiply_convert_fusion.1 = bf16[1024,1024]{0,1:T(8,128)(2,1)S(1)} fusion(bf16[1536,1024]{1,0:T(8,128)(2,1)} %bitcast.4, bf16[512,1536]{1,0:T(8,128)(2,1)} %copy-done.8, bf16[512,1536]{1,0:T(8,128)(2,1)} %copy-done.18, pred[]{:T(512)S(6)} %eq.82), kind=kOutput, calls=%fused_computation.17 | convolution fusion | flops 3237478400 | bytes 8388609 | tf_op jit(solution)/shard_map/dot_general | solution.py:100
  236.9 0.1 fusion.38
  237.1 1.4 copy-done.2
  238.5 1.3 fusion.44
  239.8 0.3 copy-done.1
  240.1 1.3 fusion.41
  241.4 0.3 copy-done
  241.7 1.3 fusion.43
  243.0 2.1 fusion.2
  245.1 1.5 fusion.42
  246.7 3.0 %fusion.11 = f32[8,256]{1,0:T(8,128)S(1)} fusion(f32[8,256,1024]{2,1,0:T(8,128)S(1)} %fusion.41, pred[256,1024]{1,0:T(8,128)(4,1)S(1)} %and_and_fusion.3, bf16[256,8,64]{0,2,1:T(8,128)(2,1)S(1)} %bitcast.108, bf16[1024,64]{0,1:T(8,128)(2,1)S(1)} %maximum_select_fusion.6, bf16[768,64]{0,1:T(8,128)(2,1)} %collective-permute-done.7), kind=kOutput, calls=%fused_computation.15 | convolution fusion | flops 277084160 | bytes 9150464 | tf_op jit(solution)/shard_map/qhd,kd->hqk/dot_general | solution.py:32
  249.7 2.9 %fusion.5 = f32[8,256]{1,0:T(8,128)S(1)} fusion(f32[8,256,1024]{2,1,0:T(8,128)S(1)} %fusion.43, pred[256,1024]{1,0:T(8,128)(4,1)S(1)} %get-tuple-element.29, bf16[256,8,64]{0,2,1:T(8,128)(2,1)S(1)} %bitcast.107, bf16[1024,64]{0,1:T(8,128)(2,1)S(1)} %maximum_select_fusion.6, bf16[768,64]{0,1:T(8,128)(2,1)} %collective-permute-done.7), kind=kOutput, calls=%fused_computation.7 | convolution fusion | flops 277084160 | bytes 9150464 | tf_op jit(solution)/shard_map/qhd,kd->hqk/dot_general | solution.py:32
  252.6 3.1 %fusion.8 = f32[8,256]{1,0:T(8,128)S(1)} fusion(f32[8,256,1024]{2,1,0:T(8,128)S(1)} %fusion.42, pred[256,1024]{1,0:T(8,128)(4,1)S(1)} %get-tuple-element.30, bf16[256,8,64]{0,2,1:T(8,128)(2,1)S(1)} %bitcast.106, bf16[1024,64]{0,1:T(8,128)(2,1)S(1)} %maximum_select_fusion.6, bf16[768,64]{0,1:T(8,128)(2,1)} %collective-permute-done.7), kind=kOutput, calls=%fused_computation.11 | convolution fusion | flops 277084160 | bytes 9150464 | tf_op jit(solution)/shard_map/qhd,kd->hqk/dot_general | solution.py:32
  255.8 0.8 collective-permute-start.8
  256.5 3.2 %collective-permute-done.8 = f32[1,4,8,256]{3,2,0,1:T(8,128)S(1)} collective-permute-done((f32[1,4,8,256]{3,2,0,1:T(8,128)S(1)}, f32[1,4,8,256]{3,2,0,1:T(8,128)S(1)}, u32[]{:S(2)}, u32[]{:S(2)}) %collective-permute-start.8) | collective-permute-done | bytes 32800 | tf_op jit(solution)/shard_map/ppermute | solution.py:21
  259.8 2.6 collective-permute-start.9
  263.0 1.6 collective-permute-done.9
  264.6 0.6 fusion.35
  265.2 0.1 reduce_max.52
  265.3 17.8 %pmax.7 = f32[32]{0:T(128)S(1)} all-reduce(f32[32]{0:T(128)S(1)} %reduce_max.52), channel_id=1, replica_groups=mesh['seq'=8,'head'=4] {'seq'}, use_global_device_ids=true, to_apply=%region_5.6 | all-reduce | flops 32 | bytes 256 | tf_op jit(solution)/shard_map/pmax | solution.py:145
  283.2 0.9 multiply_convert_fusion.5
  284.1 1.5 multiply_convert_fusion.2
  285.7 1.0 multiply_convert_fusion.4
  (64 shorter events, 0.7 us)
Async XLA Ops:
  0.6 19.8 %copy-start.5 = (bf16[192,2048]{1,0:T(8,128)(2,1)S(1)}, bf16[192,2048]{1,0:T(8,128)(2,1)}, u32[]{:S(2)}) copy-start(bf16[192,2048]{1,0:T(8,128)(2,1)} %param.13) | copy-start | bytes 2359300
  2.0 13.8 %all-to-all-start = ((s32[8,1,256]{2,1,0:T(1,128)}), s32[8,1,256]{2,1,0:T(1,128)S(1)}, u32[]{:S(2)}, u32[]{:S(2)}) async-start(s32[8,1,256]{2,1,0:T(1,128)} %stack.12), calls=%async_computation | async-start | bytes 16384 | tf_op jit(solution)/shard_map/all_to_all | solution.py:110
  16.9 28.3 %all-to-all-start.2 = ((bf16[8,64,1024]{2,1,0:T(8,128)(2,1)}), bf16[8,64,1024]{2,1,0:T(8,128)(2,1)S(1)}, u32[]{:S(2)}, u32[]{:S(2)}) async-start(bf16[8,64,1024]{2,1,0:T(8,128)(2,1)} %bitcast.7), calls=%async_computation.2 | async-start | bytes 2097152 | tf_op jit(solution)/shard_map/all_to_all | solution.py:67
  21.2 29.8 %copy-start.3 = (bf16[192,4096]{1,0:T(8,128)(2,1)S(1)}, bf16[192,4096]{1,0:T(8,128)(2,1)}, u32[]{:S(2)}) copy-start(bf16[192,4096]{1,0:T(8,128)(2,1)} %param.12) | copy-start | bytes 4718596
  45.2 1.5 copy-start.9
  46.7 40.7 %all-to-all-start.3 = ((bf16[8,192,512]{2,1,0:T(8,128)(2,1)}), bf16[8,192,512]{2,1,0:T(8,128)(2,1)}, u32[]{:S(2)}, u32[]{:S(2)}) async-start(bf16[8,192,512]{2,1,0:T(8,128)(2,1)} %bitcast.12), calls=%async_computation.3 | async-start | bytes 3145728 | tf_op jit(solution)/shard_map/all_to_all | solution.py:66
  89.5 4.6 %copy-start.16 = (bf16[256,64]{0,1:T(8,128)(2,1)S(1)}, bf16[256,64]{0,1:T(8,128)(2,1)}, u32[]{:S(2)}) copy-start(bf16[256,64]{0,1:T(8,128)(2,1)} %param.10) | copy-start | bytes 98308
  89.5 6.5 %copy-start.15 = (bf16[256,128]{1,0:T(8,128)(2,1)S(1)}, bf16[256,128]{1,0:T(8,128)(2,1)}, u32[]{:S(2)}) copy-start(bf16[256,128]{1,0:T(8,128)(2,1)} %param.9) | copy-start | bytes 196612
  89.5 12.5 %copy-start.14 = (bf16[256,384]{1,0:T(8,128)(2,1)S(1)}, bf16[256,384]{1,0:T(8,128)(2,1)}, u32[]{:S(2)}) copy-start(bf16[256,384]{1,0:T(8,128)(2,1)} %param.8) | copy-start | bytes 589828
  89.5 140.1 %all-to-all-start.1 = ((bf16[8,192,1024]{2,1,0:T(8,128)(2,1)}), bf16[8,192,1024]{2,1,0:T(8,128)(2,1)}, u32[]{:S(2)}, u32[]{:S(2)}) async-start(bf16[8,192,1024]{2,1,0:T(8,128)(2,1)} %bitcast.3), calls=%async_computation.1 | async-start | bytes 6291456 | tf_op jit(solution)/shard_map/all_to_all | solution.py:65
  94.1 69.7 %collective-permute-start.5 = (bf16[256,64]{0,1:T(8,128)(2,1)S(1)}, bf16[256,64]{0,1:T(8,128)(2,1)S(1)}, u32[]{:S(2)}, u32[]{:S(2)}) collective-permute-start(bf16[256,64]{0,1:T(8,128)(2,1)S(1)} %copy-done.16), channel_id=1, source_target_pairs={{0,4},{4,0},{8,12},{12,8},{16,20},{20,16},{24,28},{28,24},{1,5},{5... | collective-permute-start | bytes 98312 | tf_op jit(solution)/shard_map/ppermute | solution.py:21
  101.8 26.1 %collective-permute-start.2 = (bf16[256,512]{1,0:T(8,128)(2,1)S(1)}, bf16[256,512]{1,0:T(8,128)(2,1)S(1)}, u32[]{:S(2)}, u32[]{:S(2)}) collective-permute-start(bf16[256,512]{1,0:T(8,128)(2,1)S(1)} %all_gather.7), channel_id=1, source_target_pairs={{0,4},{4,0},{8,12},{12,8},{16,20},{20,16},{24,28},{28,24},{1,5},{5... | collective-permute-start | bytes 786440 | tf_op jit(solution)/shard_map/ppermute | solution.py:21
  110.6 52.2 %collective-permute-start = (bf16[256,1536]{1,0:T(8,128)(2,1)S(1)}, bf16[256,1536]{1,0:T(8,128)(2,1)S(1)}, u32[]{:S(2)}, u32[]{:S(2)}) collective-permute-start(bf16[256,1536]{1,0:T(8,128)(2,1)S(1)} %all_gather.6), channel_id=1, source_target_pairs={{0,4},{4,0},{8,12},{12,8},{16,20},{20,16},{24,28},{28,24},{1,5},{5... | collective-permute-start | bytes 2359304 | tf_op jit(solution)/shard_map/ppermute | solution.py:21
  128.2 28.1 %collective-permute-start.3 = (bf16[512,512]{1,0:T(8,128)(2,1)S(1)}, bf16[512,512]{1,0:T(8,128)(2,1)S(1)}, u32[]{:S(2)}, u32[]{:S(2)}) collective-permute-start(bf16[512,512]{1,0:T(8,128)(2,1)S(1)} %maximum_select_fusion.5), channel_id=1, source_target_pairs={{0,8},{4,12},{8,0},{12,4},{16,24},{20,28},{24,16},{28,20},{1,9},{5... | collective-permute-start | bytes 1572872 | tf_op jit(solution)/shard_map/ppermute | solution.py:21
  156.7 63.0 %copy-start.10 = (bf16[8,64,1024]{2,1,0:T(8,128)(2,1)S(1)}, bf16[8,64,1024]{2,1,0:T(8,128)(2,1)}, u32[]{:S(2)}) copy-start(bf16[8,64,1024]{2,1,0:T(8,128)(2,1)} %copy-done.9) | copy-start | bytes 3145732
  156.8 62.9 %collective-permute-start.4 = (bf16[768,512]{1,0:T(8,128)(2,1)S(1)}, bf16[768,512]{1,0:T(8,128)(2,1)S(1)}, u32[]{:S(2)}, u32[]{:S(2)}) collective-permute-start(bf16[768,512]{1,0:T(8,128)(2,1)S(1)} %slice.117), channel_id=1, source_target_pairs={{0,16},{4,20},{8,24},{12,28},{1,17},{5,21},{9,25},{13,29},{2,18},{... | collective-permute-start | bytes 2359304 | tf_op jit(solution)/shard_map/ppermute | solution.py:27
  163.4 61.4 %copy-start.8 = (bf16[512,1536]{1,0:T(8,128)(2,1)}, bf16[512,1536]{1,0:T(8,128)(2,1)S(1)}, u32[]{:S(2)}) copy-start(bf16[512,1536]{1,0:T(8,128)(2,1)S(1)} %maximum_select_fusion.1) | copy-start | bytes 4718596
  163.4 61.4 %collective-permute-start.1 = (bf16[512,1536]{1,0:T(8,128)(2,1)S(1)}, bf16[512,1536]{1,0:T(8,128)(2,1)S(1)}, u32[]{:S(2)}, u32[]{:S(2)}) collective-permute-start(bf16[512,1536]{1,0:T(8,128)(2,1)S(1)} %maximum_select_fusion.1), channel_id=1, source_target_pairs={{0,8},{4,12},{8,0},{12,4},{16,24},{20,28},{24,16},{28,20},{1,9},{5... | collective-permute-start | bytes 4718600 | tf_op jit(solution)/shard_map/ppermute | solution.py:21
  163.9 49.2 %collective-permute-start.6 = (bf16[512,64]{0,1:T(8,128)(2,1)S(1)}, bf16[512,64]{0,1:T(8,128)(2,1)S(1)}, u32[]{:S(2)}, u32[]{:S(2)}) collective-permute-start(bf16[512,64]{0,1:T(8,128)(2,1)S(1)} %maximum_select_fusion.7), channel_id=1, source_target_pairs={{0,8},{4,12},{8,0},{12,4},{16,24},{20,28},{24,16},{28,20},{1,9},{5... | collective-permute-start | bytes 196616 | tf_op jit(solution)/shard_map/ppermute | solution.py:21
  213.7 32.9 %collective-permute-start.7 = (bf16[768,64]{0,1:T(8,128)(2,1)}, bf16[768,64]{0,1:T(8,128)(2,1)}, u32[]{:S(2)}, u32[]{:S(2)}) collective-permute-start(bf16[768,64]{0,1:T(8,128)(2,1)} %slice.119), channel_id=1, source_target_pairs={{0,16},{4,20},{8,24},{12,28},{1,17},{5,21},{9,25},{13,29},{2,18},{... | collective-permute-start | bytes 294920 | tf_op jit(solution)/shard_map/ppermute | solution.py:27
  224.8 3.9 %copy-start.18 = (bf16[512,1536]{1,0:T(8,128)(2,1)}, bf16[512,1536]{1,0:T(8,128)(2,1)S(1)}, u32[]{:S(2)}) copy-start(bf16[512,1536]{1,0:T(8,128)(2,1)S(1)} %collective-permute-done.1) | copy-start | bytes 4718596
  236.9 1.6 copy-start.2
  238.5 1.6 copy-start.1
  240.1 1.6 copy-start
  241.7 1.3 copy-start.13
  245.1 1.5 copy-start.12
  246.7 3.1 %copy-start.11 = (bf16[256,512]{0,1:T(8,128)(2,1)S(1)}, bf16[256,512]{0,1:T(8,128)(2,1)}, u32[]{:S(2)}) copy-start(bf16[256,512]{0,1:T(8,128)(2,1)} %get-tuple-element.19) | copy-start | bytes 786436
  252.6 30.6 %copy-start.7 = (bf16[64,4096]{1,0:T(8,128)(2,1)S(1)}, bf16[64,4096]{1,0:T(8,128)(2,1)}, u32[]{:S(2)}) copy-start(bf16[64,4096]{1,0:T(8,128)(2,1)} %param.14) | copy-start | bytes 1572868
  252.6 31.4 %copy-start.4 = (bf16[192,4096]{1,0:T(8,128)(2,1)S(1)}, bf16[192,4096]{1,0:T(8,128)(2,1)}, u32[]{:S(2)}) copy-start(bf16[192,4096]{1,0:T(8,128)(2,1)} %param.12) | copy-start | bytes 4718596
  255.8 29.9 %copy-start.6 = (bf16[192,2048]{1,0:T(8,128)(2,1)S(1)}, bf16[192,2048]{1,0:T(8,128)(2,1)}, u32[]{:S(2)}) copy-start(bf16[192,2048]{1,0:T(8,128)(2,1)} %param.13) | copy-start | bytes 2359300
  255.8 4.0 %collective-permute-start.8 = (f32[1,4,8,256]{3,2,0,1:T(8,128)S(1)}, f32[1,4,8,256]{3,2,0,1:T(8,128)S(1)}, u32[]{:S(2)}, u32[]{:S(2)}) collective-permute-start(f32[1,4,8,256]{3,2,0,1:T(8,128)S(1)} %maximum_bitcast_fusion), channel_id=1, source_target_pairs={{0,4},{4,0},{8,12},{12,8},{16,20},{20,16},{24,28},{28,24},{1,5},{5... | collective-permute-start | bytes 98312 | tf_op jit(solution)/shard_map/ppermute | solution.py:21
  259.8 4.8 %collective-permute-start.9 = (f32[2,4,8,256]{3,2,0,1:T(8,128)S(1)}, f32[2,4,8,256]{3,2,0,1:T(8,128)S(1)}, u32[]{:S(2)}, u32[]{:S(2)}) collective-permute-start(f32[2,4,8,256]{3,2,0,1:T(8,128)S(1)} %maximum_select_fusion.8), channel_id=1, source_target_pairs={{0,8},{4,12},{8,0},{12,4},{16,24},{20,28},{24,16},{28,20},{1,9},{5... | collective-permute-start | bytes 196616 | tf_op jit(solution)/shard_map/ppermute | solution.py:21
  283.1 3.6 %copy-start.17 = (f32[32]{0:T(128)}, f32[32]{0:T(128)S(1)}, u32[]{:S(2)}) copy-start(f32[32]{0:T(128)S(1)} %pmax.7) | copy-start | bytes 388
